TPU v7x, 128 devices: a whole 4x4x4 slice. The times are simulated.
128 devices in a mesh: prow: 8 (over z_hi, y), pcol: 16 (over x, z_lo, core).
Axes of the slice: x: 4, y: 4, z: 4 (z_hi: 2, z_lo: 2; z = z_hi * 2 + z_lo), core: 2. Of those that a mesh axis runs over, the one named last changes fastest.
Arguments:
- panel_t: float32 [16, 256, 8192], P('pcol', None, 'prow'), may hold values from -0.0625 to 0.0625
- ancestor: float32 [8192, 8192], P('prow', 'pcol'), as said below
- structure: int32 [16, 32], replicated, may hold values 0 or 1
- diag_inv: float32 [16, 256, 256], P('pcol'), may hold values from -6 to 6
Outputs:
- inverse_panel: float32 [4096, 8192], P('pcol', 'prow')
- inverse_diag: float32 [16, 256, 256], P('pcol')
Inputs may be any that keep to these rules, and one draw needn't show every extreme that they name: ancestor is symmetric up to rounding.
All inputs are finite; a program needn't handle non-finite values.
Results may differ from a plain program's by a relative error of at most 0.00007.
Values sent between devices are 32-bit elements; how exact they have to be, the bound alone decides.
A program may use at most 128 MiB of HBM per device.

v0:
```python
import jax
import jax.numpy as jnp
from jax import lax
from jax.sharding import PartitionSpec as P


def copy_for_each(array, axis):
    length = lax.axis_size(axis)
    return lax.all_to_all(
        jnp.broadcast_to(array[None], (length, *array.shape)), axis, 0, 0, tiled=True
    )


def of_everyone(array, axis):
    everything = copy_for_each(array, axis)
    return jnp.sum(everything, axis=0)


def local(panel_t, ancestor, structure, diag_inv):
    local_sn = panel_t.shape[0]
    width = panel_t.shape[1]
    row_span = panel_t.shape[2]
    row_blocks = row_span // width
    col_index = lax.axis_index("pcol")
    row_index = lax.axis_index("prow")
    mine = lax.dynamic_slice(
        structure, (col_index * local_sn, row_index * row_blocks), (local_sn, row_blocks)
    )
    masked = (
        panel_t.reshape(local_sn, width, row_blocks, width)
        * mine.astype(jnp.float32)[:, None, :, None]
    )
    masked = masked.reshape(local_sn, width, row_span)
    prow_size = lax.axis_size("prow")
    rows_here = width // prow_size
    arranged = masked.reshape(local_sn, prow_size, rows_here, row_span).transpose(1, 0, 2, 3)
    gathered = lax.all_gather(arranged, "pcol", axis=1, tiled=True)
    total_nodes = gathered.shape[1]
    flat_rows = gathered.reshape(prow_size * total_nodes * rows_here, row_span)
    reduced = lax.psum_scatter(
        jnp.dot(
            flat_rows, ancestor, precision=lax.Precision.HIGHEST, preferred_element_type=jnp.float32
        ),
        "prow",
        scatter_dimension=0,
        tiled=True,
    )
    moved = lax.all_to_all(
        lax.all_to_all(reduced, "pcol", split_axis=0, concat_axis=1, tiled=True),
        "prow",
        split_axis=1,
        concat_axis=0,
        tiled=True,
    )
    summed = moved.reshape(prow_size, local_sn, rows_here, row_span).transpose(1, 0, 2, 3)
    summed = summed.reshape(local_sn * width, row_span)
    inverse_panel = -summed
    blocks = inverse_panel.reshape(local_sn, width, row_span)
    partial_diag = jnp.einsum("kbj,kcj->kbc", blocks, masked, precision=lax.Precision.HIGHEST)
    inverse_diag = diag_inv - of_everyone(partial_diag, "prow")
    return (inverse_panel, inverse_diag)


def solution(mesh):
    return jax.shard_map(
        local,
        mesh=mesh,
        in_specs=(P("pcol", None, "prow"), P("prow", "pcol"), P(), P("pcol", None, None)),
        out_specs=(P("pcol", "prow"), P("pcol", None, None)),
        check_vma=False,
    )
```

profile of v0, /device:TPU:32, one launch (start us, length us, event | category | flops | bytes accessed | tf_op | source)
XLA Modules:
  0.0 340.1 jit_solution(9076834743426126464)
XLA Ops:
  7.2 0.0 copy-start
  7.2 0.0 all-gather.2.cloned.1.call-start
  7.2 0.9 convert_bitcast_fusion
  8.1 0.1 broadcast_bitcast_fusion
  8.2 2.3 broadcast_multiply_fusion
  10.6 0.0 all-gather.2.cloned.1.call-update
  10.6 0.0 reduce-scatter.2.cloned.1.call-start
  10.6 93.6 %all-gather.2.cloned.1.call-done = f32[8,16,32,1024]{3,2,1,0:T(8,128)} async-done(((f32[8,1,32,1024]{3,2,1,0:T(8,128)}), f32[8,16,32,1024]{3,2,1,0:T(8,128)}) %all-gather.2.cloned.1.call-update) | async-done | bytes 16777232 | tf_op jit(solution)/shard_map/all_gather | solution.py:37
  104.3 0.0 copy-done
  104.3 30.3 %fusion.4 = f32[4096,512]{1,0:T(8,128)} fusion(f32[4096,1024]{1,0:T(8,128)} %bitcast.27, f32[1024,512]{1,0:T(8,128)S(1)} %copy-done), kind=kOutput, calls=%fused_computation.8 | convolution fusion | flops 25769803776 | bytes 27262976 | tf_op jit(solution)/shard_map/dot_general | solution.py:41
  134.5 0.0 reduce-scatter.2.cloned.1.call-update
  134.6 0.0 copy-start.1
  134.6 114.6 %reduce-scatter.2.cloned.1.call-done = f32[512,512]{1,0:T(8,128)} async-done(((f32[4096,512]{1,0:T(8,128)}), f32[512,512]{1,0:T(8,128)}) %reduce-scatter.2.cloned.1.call-update) | async-done | bytes 1048592 | tf_op jit(solution)/shard_map/reduce_scatter | solution.py:40
  249.1 20.5 %all_to_all.34 = f32[16,32,512]{2,1,0:T(8,128)S(1)} all-to-all(f32[16,32,512]{2,1,0:T(8,128)} %bitcast.24), channel_id=1, replica_groups=mesh['prow'=8,'pcol'=16] {'pcol'}, dimensions={0} | all-to-all | bytes 2097152 | tf_op jit(solution)/shard_map/all_to_all | solution.py:49
  269.7 1.6 copy.11
  271.2 2.5 all_to_all.28
  273.8 0.0 copy-start.3
  273.8 1.9 copy.12
  275.6 21.0 %all_to_all.35 = f32[32,8,1024]{2,0,1:T(8,128)S(1)} all-to-all(f32[32,8,1024]{2,0,1:T(8,128)S(1)} %copy.12), channel_id=1, replica_groups=mesh['prow'=8,'pcol'=16] {'prow'}, dimensions={1} | all-to-all | bytes 2097152 | tf_op jit(solution)/shard_map/all_to_all | solution.py:48
  296.7 0.1 neg.13
  296.8 0.0 copy-start.2
  296.8 1.0 copy-done.2
  297.8 0.0 copy-done.1
  297.8 1.0 fusion
  298.8 0.2 broadcast_in_dim.2
  299.0 31.7 %all_to_all.36 = f32[8,1,256,256]{3,2,1,0:T(8,128)} all-to-all(f32[8,1,256,256]{3,2,1,0:T(8,128)S(1)} %broadcast_in_dim.2), channel_id=1, replica_groups=mesh['prow'=8,'pcol'=16] {'prow'}, dimensions={0} | all-to-all | bytes 4194304 | tf_op jit(solution)/shard_map/all_to_all | solution.py:9
  330.8 1.8 reduce_sum.11
  332.5 0.0 copy-done.3
  332.5 0.7 bitcast_subtract_fusion
  (1 shorter events, 0.0 us)
Async XLA Ops:
  7.2 97.1 %copy-start = (f32[1024,512]{1,0:T(8,128)S(1)}, f32[1024,512]{1,0:T(8,128)}, u32[]{:S(2)}) copy-start(f32[1024,512]{1,0:T(8,128)} %param.5) | copy-start | bytes 6291460
  7.2 97.1 %all-gather.2.cloned.1.call-start = ((), (), s32[]{:S(2)}) async-start(), calls=%async_computation.4 | async-start | bytes 17825792 | tf_op jit(solution)/shard_map/all_gather | solution.py:37
  10.6 238.6 %reduce-scatter.2.cloned.1.call-start = ((), (), s32[]{:S(2)}) async-start(), calls=%async_computation.5 | async-start | bytes 9437184 | tf_op jit(solution)/shard_map/reduce_scatter | solution.py:40
  134.6 163.2 %copy-start.1 = (f32[1,256,1024]{2,1,0:T(8,128)S(1)}, f32[1,256,1024]{2,1,0:T(8,128)}, u32[]{:S(2)}) copy-start(f32[1,256,1024]{2,1,0:T(8,128)} %param.4) | copy-start | bytes 3145732
  273.8 58.8 %copy-start.3 = (f32[1,256,256]{2,1,0:T(8,128)S(1)}, f32[1,256,256]{2,1,0:T(8,128)}, u32[]{:S(2)}) copy-start(f32[1,256,256]{2,1,0:T(8,128)} %param.7) | copy-start | bytes 786436
  296.8 1.0 copy-start.2
Sparse Core Ops, SparseCore 0:
  10.7 93.5 all-gather.1
  134.7 114.4 reduce-scatter.1
where the time goes:
time: 340 us
  waiting for transfers between devices  208 us (61%)
  blocking collectives  73.3 us (22%)
  matrix products  31.3 us (9%)
  between operations  14.1 us (4%)
  local copies, waits for them, and re-layouts  7.22 us (2%)
  other arithmetic  5.85 us (2%)
    reduce_scatter x1, waiting for transfers between devices, local(): lax.psum_scatter(jnp.dot(flat_rows, ancestor, precision=lax.Precision.HIG...  115 us
    all_gather x1, waiting for transfers between devices, local(): gathered = lax.all_gather(arranged, 'pcol', axis=1, tiled=True)  93.6 us
    all_to_all x1, blocking collectives, copy_for_each(): lax.all_to_all(jnp.broadcast_to(array[None], (length, *array.shape)), axi...  31.7 us
    dot_general x1, matrix products, local(): jnp.dot(flat_rows, ancestor, precision=lax.Precision.HIGHEST, preferred_e...  30.3 us
    all_to_all x1, blocking collectives, local(): lax.all_to_all(lax.all_to_all(reduced, 'pcol', split_axis=0, concat_axis=...  21 us
    all_to_all x1, blocking collectives, local(): lax.all_to_all(reduced, 'pcol', split_axis=0, concat_axis=1, tiled=True)  20.5 us
  transfers between devices with their start and end apart: 2, of which 2 were waited for; matrix products, arithmetic and copies ran while one was open for 0% of the time, Pallas kernels for 0%

commit v1 on v0

--- a/solution.py
+++ b/solution.py
@@ -34,7 +34,10 @@
     prow_size = lax.axis_size("prow")
     rows_here = width // prow_size
     arranged = masked.reshape(local_sn, prow_size, rows_here, row_span).transpose(1, 0, 2, 3)
-    gathered = lax.all_gather(arranged, "pcol", axis=1, tiled=True)
+    gathered = jnp.concatenate(
+        lax.all_to_all(jnp.stack([arranged for _ in range(lax.axis_size("pcol"))]), "pcol", 0, 0),
+        axis=1,
+    )
     total_nodes = gathered.shape[1]
     flat_rows = gathered.reshape(prow_size * total_nodes * rows_here, row_span)
     reduced = lax.psum_scatter(

time: 340 us -> 441 us (1.30)
  blocking collectives: 73.3 us -> 262 us
  waiting for transfers between devices: 208 us -> 116 us
  local copies, waits for them, and re-layouts: 7.22 us -> 12.6 us
    all_to_all x0 -> x1, blocking collectives: none -> 189 us  [local(): lax.all_to_all(jnp.stack([arranged for _ in range(lax.axis_size('pcol'))]...]
    all_gather x1 -> x0, waiting for transfers between devices: 93.6 us -> none  [local(): gathered = lax.all_gather(arranged, 'pcol', axis=1, tiled=True)]
  transfers between devices with their start and end apart: 2 -> 1, of which waited for: 2 -> 1; matrix products, arithmetic and copies ran while one was open for 0% -> 0% of each run, Pallas kernels for 0% -> 0%
where the time goes in v1:
time: 441 us
  blocking collectives  262 us (59%)
  waiting for transfers between devices  116 us (26%)
  matrix products  29.7 us (7%)
  between operations  14.1 us (3%)
  local copies, waits for them, and re-layouts  12.6 us (3%)
  other arithmetic  5.85 us (1%)
    all_to_all x1, blocking collectives, local(): lax.all_to_all(jnp.stack([arranged for _ in range(lax.axis_size('pcol'))]...  189 us
    reduce_scatter x1, waiting for transfers between devices, local(): lax.psum_scatter(jnp.dot(flat_rows, ancestor, precision=lax.Precision.HIG...  116 us
    all_to_all x1, blocking collectives, copy_for_each(): lax.all_to_all(jnp.broadcast_to(array[None], (length, *array.shape)), axi...  31.7 us
    dot_general x1, matrix products, local(): jnp.dot(flat_rows, ancestor, precision=lax.Precision.HIGHEST, preferred_e...  28.6 us
    all_to_all x1, blocking collectives, local(): lax.all_to_all(lax.all_to_all(reduced, 'pcol', split_axis=0, concat_axis=...  21 us
    all_to_all x1, blocking collectives, local(): lax.all_to_all(reduced, 'pcol', split_axis=0, concat_axis=1, tiled=True)  20.5 us
  transfers between devices with their start and end apart: 1, of which 1 were waited for; matrix products, arithmetic and copies ran while one was open for 0% of the time, Pallas kernels for 0%

profile of v1, /device:TPU:32, one launch (start us, length us, event | category | flops | bytes accessed | tf_op | source)
XLA Modules:
  0.0 440.7 jit_solution(8418309956856110937)
XLA Ops:
  7.2 0.0 copy-start
  7.2 0.0 reduce-scatter.2.cloned.1.call-start
  7.2 0.9 convert_bitcast_fusion
  8.1 0.1 broadcast_bitcast_fusion
  8.2 2.3 broadcast_multiply_fusion
  10.6 3.4 stack.3
  14.0 188.9 %all_to_all.39 = f32[16,8,1,32,1024]{4,3,1,2,0:T(8,128)S(1)} all-to-all(f32[16,8,1,32,1024]{4,3,1,2,0:T(8,128)S(1)} %stack.3), channel_id=1, replica_groups=mesh['prow'=8,'pcol'=16] {'pcol'}, dimensions={0} | all-to-all | bytes 33554432 | tf_op jit(solution)/shard_map/all_to_all | solution.py:38
  202.9 1.9 copy.12
  204.8 0.0 copy-done
  204.8 28.6 %fusion.4 = f32[4096,512]{1,0:T(8,128)} fusion(f32[4096,1024]{1,0:T(8,128)S(1)} %bitcast.22, f32[1024,512]{1,0:T(8,128)S(1)} %copy-done), kind=kOutput, calls=%fused_computation.8 | convolution fusion | flops 25769803776 | bytes 27262976 | tf_op jit(solution)/shard_map/dot_general | solution.py:44
  233.4 0.0 reduce-scatter.2.cloned.1.call-update
  233.5 0.0 copy-start.1
  233.5 116.2 %reduce-scatter.2.cloned.1.call-done = f32[512,512]{1,0:T(8,128)} async-done(((f32[4096,512]{1,0:T(8,128)}), f32[512,512]{1,0:T(8,128)}) %reduce-scatter.2.cloned.1.call-update) | async-done | bytes 1048592 | tf_op jit(solution)/shard_map/reduce_scatter | solution.py:43
  349.7 20.5 %all_to_all.40 = f32[16,32,512]{2,1,0:T(8,128)S(1)} all-to-all(f32[16,32,512]{2,1,0:T(8,128)} %bitcast.27), channel_id=1, replica_groups=mesh['prow'=8,'pcol'=16] {'pcol'}, dimensions={0} | all-to-all | bytes 2097152 | tf_op jit(solution)/shard_map/all_to_all | solution.py:52
  370.2 1.6 copy.13
  371.8 2.5 all_to_all.32
  374.4 0.0 copy-start.3
  374.4 1.9 copy.14
  376.2 21.0 %all_to_all.41 = f32[32,8,1024]{2,0,1:T(8,128)S(1)} all-to-all(f32[32,8,1024]{2,0,1:T(8,128)S(1)} %copy.14), channel_id=1, replica_groups=mesh['prow'=8,'pcol'=16] {'prow'}, dimensions={1} | all-to-all | bytes 2097152 | tf_op jit(solution)/shard_map/all_to_all | solution.py:51
  397.2 0.1 neg.13
  397.4 0.0 copy-start.2
  397.4 1.0 copy-done.2
  398.3 0.0 copy-done.1
  398.3 1.0 fusion
  399.4 0.2 broadcast_in_dim.2
  399.6 31.7 %all_to_all.42 = f32[8,1,256,256]{3,2,1,0:T(8,128)} all-to-all(f32[8,1,256,256]{3,2,1,0:T(8,128)S(1)} %broadcast_in_dim.2), channel_id=1, replica_groups=mesh['prow'=8,'pcol'=16] {'prow'}, dimensions={0} | all-to-all | bytes 4194304 | tf_op jit(solution)/shard_map/all_to_all | solution.py:9
  431.3 1.8 reduce_sum.11
  433.1 0.0 copy-done.3
  433.1 0.7 bitcast_subtract_fusion
  (1 shorter events, 0.0 us)
Async XLA Ops:
  7.2 197.6 %copy-start = (f32[1024,512]{1,0:T(8,128)S(1)}, f32[1024,512]{1,0:T(8,128)}, u32[]{:S(2)}) copy-start(f32[1024,512]{1,0:T(8,128)} %param.5) | copy-start | bytes 6291460
  7.2 342.5 %reduce-scatter.2.cloned.1.call-start = ((), (), s32[]{:S(2)}) async-start(), calls=%async_computation.5 | async-start | bytes 9437184 | tf_op jit(solution)/shard_map/reduce_scatter | solution.py:43
  233.5 164.9 %copy-start.1 = (f32[1,256,1024]{2,1,0:T(8,128)S(1)}, f32[1,256,1024]{2,1,0:T(8,128)}, u32[]{:S(2)}) copy-start(f32[1,256,1024]{2,1,0:T(8,128)} %param.4) | copy-start | bytes 3145732
  374.4 58.7 %copy-start.3 = (f32[1,256,256]{2,1,0:T(8,128)S(1)}, f32[1,256,256]{2,1,0:T(8,128)}, u32[]{:S(2)}) copy-start(f32[1,256,256]{2,1,0:T(8,128)} %param.7) | copy-start | bytes 786436
  397.4 1.0 copy-start.2
Sparse Core Ops, SparseCore 0:
  233.6 116.0 reduce-scatter.1
